TPU v7x, 128 devices: a whole 4x4x4 slice. The times are simulated.
128 devices in a mesh: layer: 2 (over core), expert: 16 (over y, x), matrix: 4 (over z).
Axes of the slice: x: 4, y: 4, z: 4, core: 2. Of those that a mesh axis runs over, the one named last changes fastest.
Arguments:
- grads: float32 [32, 1, 2048, 768], P(('layer', 'expert'), None, 'matrix'), parts along dimension 0, may hold values from -6 to 6
- basis_out: float32 [32, 2048, 2048], P('layer', None, ('expert', 'matrix')), parts along dimension 0, may hold values from -0.125 to 0.125
- basis_in: float32 [32, 768, 768], P('layer', ('expert', 'matrix')), parts along dimension 0, may hold values from -0.21875 to 0.21875
- eigvals: float32 [32, 2048, 768], P('layer', ('expert', 'matrix')), parts along dimension 0, may hold values from 0.001 to 1
- counts: int32 [32], P(('layer', 'expert')), parts along dimension 0, may hold values from 0 to 1, as said below
- slot_query: int32 [32, 1], P(('layer', 'expert')), parts along dimension 0, may hold values from 0 to 31
Outputs:
- precond: float32 [32, 1, 2048, 768], P(('layer', 'expert'), None, 'matrix'), parts along dimension 0
- scores: float32 [64], P('layer'), parts along dimension 0
There are 2 independent parts, one for each index of `layer`. A program takes and returns all parts, laid end to end along the dimension named above; each array names one. Nothing has to cross between parts.
Inputs may be any that keep to these rules, and one draw needn't show every extreme that they name: `counts`: some expert has no live slot and some expert has all 1.
All inputs are finite; a program needn't handle non-finite values.
Results may differ from a plain program's by a relative error of at most 0.0003.
Values sent between devices are 32-bit elements; how exact they have to be, the bound alone decides.
A program may use at most 64 MiB of HBM per device.

v0:
```python
import jax
import jax.numpy as jnp
from jax import lax
from jax.sharding import PartitionSpec as P

QUERIES = 32
damping_fixed = 0.05
highest = lax.Precision.HIGHEST


def shards(grads, basis_out, basis_in, eigvals, counts, slot_query):
    capacity = grads.shape[1]
    own_rows = grads.shape[2]
    in_width = grads.shape[3]
    groups = lax.axis_size("matrix")
    columns = lax.all_to_all(basis_out, "expert", split_axis=0, concat_axis=2, tiled=True)[0]
    scales, inner = (
        lax.all_to_all(eigvals, "expert", split_axis=0, concat_axis=1, tiled=True),
        lax.all_to_all(basis_in, "expert", split_axis=0, concat_axis=1, tiled=True),
    )
    inner = lax.all_gather(inner, "matrix", axis=1, tiled=True)[0]
    sources = lax.axis_size("expert")
    inner = inner.reshape(groups, sources, -1, in_width).transpose(1, 0, 2, 3).reshape(-1, in_width)
    divisor = scales[0] + damping_fixed
    live_count = counts[0]
    queries = slot_query[0]
    local_rows = grads[0]
    slot_ids = jnp.arange(capacity, dtype=jnp.int32)
    live = (slot_ids < live_count).astype(jnp.float32)
    rotated = jnp.einsum(
        "ik,if->kf",
        columns,
        lax.all_gather(local_rows[0], "matrix", axis=0, tiled=True),
        precision=highest,
    )
    rotated = jnp.dot(rotated, inner, precision=highest)
    scaled = rotated / divisor
    back = jnp.einsum("kg,hg->kh", scaled, inner, precision=highest)

    def project_one(start, amount, back=back):
        return jnp.dot(columns, back, precision=highest)

    result = lax.psum_scatter(
        project_one(jnp.int32(0), own_rows * lax.axis_size("matrix")),
        "matrix",
        scatter_dimension=0,
        tiled=True,
    )
    results = [result * live[0]]
    precond = jnp.stack(results)
    values = jnp.sum(local_rows * precond, axis=(1, 2)) / (own_rows * groups * in_width)
    targets = jnp.arange(QUERIES, dtype=jnp.int32)
    onehot = (queries[:, None] == targets[None, :]).astype(jnp.float32)
    partial_scores = jnp.sum(values[:, None] * onehot, axis=0)
    scores = lax.psum(partial_scores, ("expert", "matrix"))
    return (precond[None], scores)


def solution(mesh):
    in_specs = (
        P(("layer", "expert"), None, "matrix", None),
        P("layer", None, ("expert", "matrix")),
        P("layer", ("expert", "matrix"), None),
        P("layer", ("expert", "matrix"), None),
        P(("layer", "expert")),
        P(("layer", "expert"), None),
    )
    out_specs = (P(("layer", "expert"), None, "matrix", None), P("layer"))
    return jax.shard_map(shards, mesh=mesh, in_specs=in_specs, out_specs=out_specs, check_vma=False)
```

profile of v0, /device:TPU:0, one launch (start us, length us, event | category | flops | bytes accessed | tf_op | source)
XLA Modules:
  0.0 419.3 jit_solution(11684869709950085901)
XLA Ops:
  7.2 1.4 copy.14
  8.6 21.3 %all_to_all.36 = f32[16,12,768]{2,1,0:T(8,128)S(1)} all-to-all(f32[16,12,768]{2,1,0:T(8,128)S(1)} %copy.14), channel_id=1, replica_groups=mesh['layer'=2,'expert'=16,'matrix'=4] {'expert'}, dimensions={0} | all-to-all | bytes 1179648 | tf_op jit(solution)/shard_map/all_to_all | solution.py:19
  29.9 0.9 all_to_all.31
  30.9 0.0 all-gather.6.cloned.1.call-start
  30.9 0.7 all-gather.6.cloned.1.call-update
  31.6 25.2 %all_to_all.37 = f32[16,32,768]{2,1,0:T(8,128)S(1)} all-to-all(f32[16,32,768]{2,1,0:T(8,128)S(1)} %copy-done.2), channel_id=1, replica_groups=mesh['layer'=2,'expert'=16,'matrix'=4] {'expert'}, dimensions={0} | all-to-all | bytes 3145728 | tf_op jit(solution)/shard_map/all_to_all | solution.py:18
  56.8 4.5 %all-to-all-start = ((f32[16,2048,32]{1,2,0:T(8,128)}), f32[16,2048,32]{1,2,0:T(8,128)}, u32[]{:S(2)}, u32[]{:S(2)}) async-start(f32[16,2048,32]{1,2,0:T(8,128)} %param.7), calls=%async_computation | async-start | bytes 8388608 | tf_op jit(solution)/shard_map/all_to_all | solution.py:16
  61.3 0.0 reduce-scatter.2.cloned.1.call-start
  61.4 1.3 broadcast_add_fusion
  62.7 2.4 reshape_squeeze.3
  65.1 2.0 copy.15
  67.2 2.6 reshape.33
  69.8 51.2 %all-to-all-done = f32[16,2048,32]{1,2,0:T(8,128)} async-done(((f32[16,2048,32]{1,2,0:T(8,128)}), f32[16,2048,32]{1,2,0:T(8,128)}, u32[]{:S(2)}, u32[]{:S(2)}) %all-to-all-start) | async-done | bytes 4194336 | tf_op jit(solution)/shard_map/all_to_all | solution.py:16
  121.0 9.2 %all-gather.6.cloned.1.call-done = f32[1,1,2048,768]{3,2,1,0:T(8,128)} async-done(((f32[1,1,512,768]{3,2,1,0:T(8,128)}), f32[1,1,2048,768]{3,2,1,0:T(8,128)}) %all-gather.6.cloned.1.call-update) | async-done | bytes 6291472 | tf_op jit(solution)/shard_map/all_gather | solution.py:33
  130.1 13.4 %fusion = f32[512,768]{1,0:T(8,128)S(1)} fusion(f32[2048,512]{0,1:T(8,128)} %bitcast.2, f32[1,1,2048,768]{3,2,1,0:T(8,128)} %all-gather.6.cloned.1.call-done), kind=kOutput, calls=%fused_computation | convolution fusion | flops 9663676416 | bytes 12058624 | tf_op jit(solution)/shard_map/ik,if->kf/dot_general | solution.py:30
  143.5 4.1 bitcast_divide_fusion
  147.6 4.0 fusion.3
  151.6 14.2 %convolution_bitcast_fusion = f32[2048,768]{0,1:T(8,128)} fusion(f32[512,768]{1,0:T(8,128)S(1)} %fusion.3, f32[2048,512]{0,1:T(8,128)} %bitcast.2), kind=kOutput, calls=%fused_computation.2 | convolution fusion | flops 9663676416 | bytes 12058624 | tf_op jit(solution)/shard_map/dot_general | solution.py:41
  165.8 1.4 copy-done
  167.2 0.5 copy.16
  168.9 61.7 %reduce-scatter.2.cloned.1.call-done = f32[512,768]{0,1:T(8,128)} async-done(((f32[2048,768]{0,1:T(8,128)}), f32[512,768]{0,1:T(8,128)}) %reduce-scatter.2.cloned.1.call-update) | async-done | bytes 1572880 | tf_op jit(solution)/shard_map/reduce_scatter | solution.py:43
  230.6 2.5 fusion.2
  233.1 1.6 copy.17
  235.5 177.3 %psum.7 = f32[32]{0:T(128)} all-reduce(f32[32]{0:T(128)S(1)} %compare_select_fusion), channel_id=1, replica_groups=mesh['layer'=2,'expert'=16,'matrix'=4] {'expert','matrix'}, use_global_device_ids=true, to_apply=%region_2.0 | all-reduce | flops 32 | bytes 256 | tf_op jit(solution)/shard_map/psum | solution.py:55
  (10 shorter events, 0.1 us)
Async XLA Ops:
  7.2 55.5 %all-gather.4.cloned.1.call-start = ((), (), s32[]{:S(2)}) async-start(), calls=%async_computation.4 | async-start | bytes 2949120 | tf_op jit(solution)/shard_map/all_gather | solution.py:21
  29.9 1.7 copy-start.2
  30.9 99.2 %all-gather.6.cloned.1.call-start = ((), (), s32[]{:S(2)}) async-start(), calls=%async_computation.6 | async-start | bytes 7864320 | tf_op jit(solution)/shard_map/all_gather | solution.py:33
  56.8 64.2 %all-to-all-start = ((f32[16,2048,32]{1,2,0:T(8,128)}), f32[16,2048,32]{1,2,0:T(8,128)}, u32[]{:S(2)}, u32[]{:S(2)}) async-start(f32[16,2048,32]{1,2,0:T(8,128)} %param.7), calls=%async_computation | async-start | bytes 8388608 | tf_op jit(solution)/shard_map/all_to_all | solution.py:16
  61.3 169.3 %reduce-scatter.2.cloned.1.call-start = ((), (), s32[]{:S(2)}) async-start(), calls=%async_computation.5 | async-start | bytes 7864320 | tf_op jit(solution)/shard_map/reduce_scatter | solution.py:43
  130.1 13.4 %copy-start.1 = (f32[16,32,768]{2,1,0:T(8,128)S(1)}, f32[16,32,768]{2,1,0:T(8,128)}, u32[]{:S(2)}) copy-start(f32[16,32,768]{2,1,0:T(8,128)} %broadcast_add_fusion) | copy-start | bytes 4718596
  165.8 1.4 copy-start
Sparse Core Ops, SparseCore 0:
  31.0 31.6 all-gather.3
  64.3 65.7 all-gather.5
  165.9 64.6 reduce-scatter.1
where the time goes:
time: 420 us; the launch traced here: 419 us
  blocking collectives  224 us (53%)
  waiting for transfers between devices  123 us (29%)
  matrix products  35.6 us (8%)
  between operations  15.8 us (4%)
  local copies, waits for them, and re-layouts  12.9 us (3%)
  starting transfers between devices  4.66 us (1%)
    psum x1, blocking collectives, shards(): scores = lax.psum(partial_scores, ('expert', 'matrix'))  177 us
    reduce_scatter x1, waiting for transfers between devices, shards(): lax.psum_scatter(project_one(jnp.int32(0), own_rows * lax.axis_size('matr...  61.7 us
    all_to_all x1, waiting for transfers between devices, shards(): lax.all_to_all(basis_out, 'expert', split_axis=0, concat_axis=2, tiled=True)  51.2 us
    all_to_all x1, blocking collectives, shards(): lax.all_to_all(eigvals, 'expert', split_axis=0, concat_axis=1, tiled=True)  25.2 us
    all_to_all x1, blocking collectives, shards(): lax.all_to_all(basis_in, 'expert', split_axis=0, concat_axis=1, tiled=True)  21.3 us
    dot_general x1, matrix products, project_one(): return jnp.dot(columns, back, precision=highest)  14.2 us
    dot_general x1, matrix products, shards(): jnp.einsum('ik,if->kf', columns, lax.all_gather(local_rows[0], 'matrix',...  13.4 us
    all_gather x1, waiting for transfers between devices, shards(): lax.all_gather(local_rows[0], 'matrix', axis=0, tiled=True)  9.16 us
  transfers between devices with their start and end apart: 4, of which 3 were waited for; matrix products, arithmetic and copies ran while one was open for 2% of the time, Pallas kernels for 0%

commit v1 on v0

--- a/solution.py
+++ b/solution.py
@@ -52,7 +52,8 @@
     targets = jnp.arange(QUERIES, dtype=jnp.int32)
     onehot = (queries[:, None] == targets[None, :]).astype(jnp.float32)
     partial_scores = jnp.sum(values[:, None] * onehot, axis=0)
-    scores = lax.psum(partial_scores, ("expert", "matrix"))
+    half = lax.psum(partial_scores, "expert")
+    scores = lax.psum(half, "matrix")
     return (precond[None], scores)
 
 

time: 420 us -> 292 us (0.70)
  blocking collectives: 224 us -> 95.7 us
    psum x1 -> x2, blocking collectives: 177 us -> 49.3 us  [the longest x1 40.3 us: shards(): half = lax.psum(partial_scores, 'expert')]
  transfers between devices with their start and end apart: 4 -> 4, of which waited for: 3 -> 3; matrix products, arithmetic and copies ran while one was open for 2% -> 3% of each run, Pallas kernels for 0% -> 0%
where the time goes in v1:
time: 292 us; the launch traced here: 291 us
  waiting for transfers between devices  123 us (42%)
  blocking collectives  95.7 us (33%)
  matrix products  35.5 us (12%)
  between operations  15.7 us (5%)
  local copies, waits for them, and re-layouts  12.9 us (4%)
  starting transfers between devices  4.67 us (2%)
  other arithmetic  3.77 us (1%)
    reduce_scatter x1, waiting for transfers between devices, shards(): lax.psum_scatter(project_one(jnp.int32(0), own_rows * lax.axis_size('matr...  61.7 us
    all_to_all x1, waiting for transfers between devices, shards(): lax.all_to_all(basis_out, 'expert', split_axis=0, concat_axis=2, tiled=True)  51.2 us
    psum x1, blocking collectives, shards(): half = lax.psum(partial_scores, 'expert')  40.3 us
    all_to_all x1, blocking collectives, shards(): lax.all_to_all(eigvals, 'expert', split_axis=0, concat_axis=1, tiled=True)  25.2 us
    all_to_all x1, blocking collectives, shards(): lax.all_to_all(basis_in, 'expert', split_axis=0, concat_axis=1, tiled=True)  21.3 us
    dot_general x1, matrix products, project_one(): return jnp.dot(columns, back, precision=highest)  14.1 us
    dot_general x1, matrix products, shards(): jnp.einsum('ik,if->kf', columns, lax.all_gather(local_rows[0], 'matrix',...  13.4 us
    all_gather x1, waiting for transfers between devices, shards(): lax.all_gather(local_rows[0], 'matrix', axis=0, tiled=True)  9.14 us
  transfers between devices with their start and end apart: 4, of which 3 were waited for; matrix products, arithmetic and copies ran while one was open for 3% of the time, Pallas kernels for 0%

profile of v1, /device:TPU:0, one launch (start us, length us, event | category | flops | bytes accessed | tf_op | source)
XLA Modules:
  0.0 291.1 jit_solution(15411120259842075962)
XLA Ops:
  7.2 1.4 copy.14
  8.6 21.3 %all_to_all.36 = f32[16,12,768]{2,1,0:T(8,128)S(1)} all-to-all(f32[16,12,768]{2,1,0:T(8,128)S(1)} %copy.14), channel_id=1, replica_groups=mesh['layer'=2,'expert'=16,'matrix'=4] {'expert'}, dimensions={0} | all-to-all | bytes 1179648 | tf_op jit(solution)/shard_map/all_to_all | solution.py:19
  29.9 0.9 all_to_all.31
  30.9 0.7 all-gather.6.cloned.1.call-update
  31.7 25.2 %all_to_all.37 = f32[16,32,768]{2,1,0:T(8,128)S(1)} all-to-all(f32[16,32,768]{2,1,0:T(8,128)S(1)} %copy-done.2), channel_id=1, replica_groups=mesh['layer'=2,'expert'=16,'matrix'=4] {'expert'}, dimensions={0} | all-to-all | bytes 3145728 | tf_op jit(solution)/shard_map/all_to_all | solution.py:18
  56.8 4.6 %all-to-all-start = ((f32[16,2048,32]{1,2,0:T(8,128)}), f32[16,2048,32]{1,2,0:T(8,128)}, u32[]{:S(2)}, u32[]{:S(2)}) async-start(f32[16,2048,32]{1,2,0:T(8,128)} %param.7), calls=%async_computation | async-start | bytes 8388608 | tf_op jit(solution)/shard_map/all_to_all | solution.py:16
  61.4 0.0 reduce-scatter.2.cloned.1.call-start
  61.4 1.3 broadcast_add_fusion
  62.7 2.4 reshape_squeeze.3
  65.2 2.0 copy.15
  67.2 2.6 reshape.33
  69.8 51.2 %all-to-all-done = f32[16,2048,32]{1,2,0:T(8,128)} async-done(((f32[16,2048,32]{1,2,0:T(8,128)}), f32[16,2048,32]{1,2,0:T(8,128)}, u32[]{:S(2)}, u32[]{:S(2)}) %all-to-all-start) | async-done | bytes 4194336 | tf_op jit(solution)/shard_map/all_to_all | solution.py:16
  121.0 9.1 %all-gather.6.cloned.1.call-done = f32[1,1,2048,768]{3,2,1,0:T(8,128)} async-done(((f32[1,1,512,768]{3,2,1,0:T(8,128)}), f32[1,1,2048,768]{3,2,1,0:T(8,128)}) %all-gather.6.cloned.1.call-update) | async-done | bytes 6291472 | tf_op jit(solution)/shard_map/all_gather | solution.py:33
  130.1 13.4 %fusion = f32[512,768]{1,0:T(8,128)S(1)} fusion(f32[2048,512]{0,1:T(8,128)} %bitcast.2, f32[1,1,2048,768]{3,2,1,0:T(8,128)} %all-gather.6.cloned.1.call-done), kind=kOutput, calls=%fused_computation | convolution fusion | flops 9663676416 | bytes 12058624 | tf_op jit(solution)/shard_map/ik,if->kf/dot_general | solution.py:30
  143.5 4.1 %bitcast_divide_fusion = f32[512,768]{1,0:T(8,128)S(1)} fusion(f32[16,32,768]{2,1,0:T(8,128)S(1)} %copy-done.1, f32[512,768]{1,0:T(8,128)S(1)} %fusion, f32[768,768]{1,0:T(8,128)S(1)} %reshape.33), kind=kOutput, calls=%fused_computation.5 | convolution fusion | flops 3624271872 | bytes 7077888 | tf_op jit(solution)/shard_map/dot_general | solution.py:36
  147.6 4.0 %fusion.3 = f32[512,768]{1,0:T(8,128)S(1)} fusion(f32[512,768]{1,0:T(8,128)S(1)} %bitcast_divide_fusion, f32[768,768]{1,0:T(8,128)S(1)} %reshape.33), kind=kOutput, calls=%fused_computation.9 | convolution fusion | flops 3623878656 | bytes 5505024 | tf_op jit(solution)/shard_map/kg,hg->kh/dot_general | solution.py:38
  151.6 14.1 %convolution_bitcast_fusion = f32[2048,768]{0,1:T(8,128)} fusion(f32[512,768]{1,0:T(8,128)S(1)} %fusion.3, f32[2048,512]{0,1:T(8,128)} %bitcast.2), kind=kOutput, calls=%fused_computation.2 | convolution fusion | flops 9663676416 | bytes 12058624 | tf_op jit(solution)/shard_map/dot_general | solution.py:41
  165.7 1.4 copy-done
  167.1 0.5 copy.16
  168.9 61.7 %reduce-scatter.2.cloned.1.call-done = f32[512,768]{0,1:T(8,128)} async-done(((f32[2048,768]{0,1:T(8,128)}), f32[512,768]{0,1:T(8,128)}) %reduce-scatter.2.cloned.1.call-update) | async-done | bytes 1572880 | tf_op jit(solution)/shard_map/reduce_scatter | solution.py:43
  230.6 2.5 fusion.2
  233.0 1.6 copy.17
  235.3 40.3 %psum.14 = f32[32]{0:T(128)S(1)} all-reduce(f32[32]{0:T(128)S(1)} %compare_select_fusion), channel_id=1, replica_groups=mesh['layer'=2,'expert'=16,'matrix'=4] {'expert'}, use_global_device_ids=true, to_apply=%region_2.0 | all-reduce | flops 32 | bytes 256 | tf_op jit(solution)/shard_map/psum | solution.py:55
  275.6 9.0 %psum.15 = f32[32]{0:T(128)} all-reduce(f32[32]{0:T(128)S(1)} %psum.14), channel_id=1, replica_groups=mesh['layer'=2,'expert'=16,'matrix'=4] {'matrix'}, use_global_device_ids=true, to_apply=%region_3.0 | all-reduce | flops 32 | bytes 256 | tf_op jit(solution)/shard_map/psum | solution.py:56
  (11 shorter events, 0.1 us)
Async XLA Ops:
  7.2 55.6 %all-gather.4.cloned.1.call-start = ((), (), s32[]{:S(2)}) async-start(), calls=%async_computation.4 | async-start | bytes 2949120 | tf_op jit(solution)/shard_map/all_gather | solution.py:21
  29.9 1.7 copy-start.2
  30.9 99.2 %all-gather.6.cloned.1.call-start = ((), (), s32[]{:S(2)}) async-start(), calls=%async_computation.6 | async-start | bytes 7864320 | tf_op jit(solution)/shard_map/all_gather | solution.py:33
  56.8 64.2 %all-to-all-start = ((f32[16,2048,32]{1,2,0:T(8,128)}), f32[16,2048,32]{1,2,0:T(8,128)}, u32[]{:S(2)}, u32[]{:S(2)}) async-start(f32[16,2048,32]{1,2,0:T(8,128)} %param.7), calls=%async_computation | async-start | bytes 8388608 | tf_op jit(solution)/shard_map/all_to_all | solution.py:16
  61.4 169.2 %reduce-scatter.2.cloned.1.call-start = ((), (), s32[]{:S(2)}) async-start(), calls=%async_computation.5 | async-start | bytes 7864320 | tf_op jit(solution)/shard_map/reduce_scatter | solution.py:43
  130.1 13.4 %copy-start.1 = (f32[16,32,768]{2,1,0:T(8,128)S(1)}, f32[16,32,768]{2,1,0:T(8,128)}, u32[]{:S(2)}) copy-start(f32[16,32,768]{2,1,0:T(8,128)} %broadcast_add_fusion) | copy-start | bytes 4718596
  165.7 1.4 copy-start
Sparse Core Ops, SparseCore 0:
  31.0 31.6 all-gather.3
  64.3 65.7 all-gather.5
  165.8 64.6 reduce-scatter.1

commit v2 on v0

--- a/solution.py
+++ b/solution.py
@@ -2,6 +2,7 @@
 import jax.numpy as jnp
 from jax import lax
 from jax.sharding import PartitionSpec as P
+from jax.lax import all_gather
 
 QUERIES = 32
 damping_fixed = 0.05
@@ -52,7 +53,7 @@
     targets = jnp.arange(QUERIES, dtype=jnp.int32)
     onehot = (queries[:, None] == targets[None, :]).astype(jnp.float32)
     partial_scores = jnp.sum(values[:, None] * onehot, axis=0)
-    scores = lax.psum(partial_scores, ("expert", "matrix"))
+    scores = jnp.sum(all_gather(partial_scores, ("expert", "matrix")), axis=0)
     return (precond[None], scores)
 
 

time: 420 us -> 417 us (level)
    psum x1 -> x0, blocking collectives: 177 us -> none  [shards(): scores = lax.psum(partial_scores, ('expert', 'matrix'))]
    all_gather x0 -> x1, blocking collectives: none -> 174 us  [shards(): scores = jnp.sum(all_gather(partial_scores, ('expert', 'matrix')), axis=0)]
where the time goes in v2:
time: 417 us
  blocking collectives  221 us (53%)
  waiting for transfers between devices  123 us (29%)
  matrix products  35.6 us (9%)
  between operations  15.8 us (4%)
  local copies, waits for them, and re-layouts  12.9 us (3%)
  starting transfers between devices  4.66 us (1%)
  other arithmetic  4.42 us (1%)
    all_gather x1, blocking collectives, shards(): scores = jnp.sum(all_gather(partial_scores, ('expert', 'matrix')), axis=0)  174 us
    reduce_scatter x1, waiting for transfers between devices, shards(): lax.psum_scatter(project_one(jnp.int32(0), own_rows * lax.axis_size('matr...  61.7 us
    all_to_all x1, waiting for transfers between devices, shards(): lax.all_to_all(basis_out, 'expert', split_axis=0, concat_axis=2, tiled=True)  51.2 us
    all_to_all x1, blocking collectives, shards(): lax.all_to_all(eigvals, 'expert', split_axis=0, concat_axis=1, tiled=True)  25.2 us
    all_to_all x1, blocking collectives, shards(): lax.all_to_all(basis_in, 'expert', split_axis=0, concat_axis=1, tiled=True)  21.3 us
    dot_general x1, matrix products, project_one(): return jnp.dot(columns, back, precision=highest)  14.2 us
    dot_general x1, matrix products, shards(): jnp.einsum('ik,if->kf', columns, lax.all_gather(local_rows[0], 'matrix',...  13.4 us
    all_gather x1, waiting for transfers between devices, shards(): lax.all_gather(local_rows[0], 'matrix', axis=0, tiled=True)  9.16 us
  transfers between devices with their start and end apart: 4, of which 3 were waited for; matrix products, arithmetic and copies ran while one was open for 2% of the time, Pallas kernels for 0%

profile of v2, /device:TPU:0, one launch (start us, length us, event | category | flops | bytes accessed | tf_op | source)
XLA Modules:
  0.0 417.0 jit_solution(9197636823018354797)
XLA Ops:
  7.2 1.4 copy.14
  8.6 21.3 %all_to_all.36 = f32[16,12,768]{2,1,0:T(8,128)S(1)} all-to-all(f32[16,12,768]{2,1,0:T(8,128)S(1)} %copy.14), channel_id=1, replica_groups=mesh['layer'=2,'expert'=16,'matrix'=4] {'expert'}, dimensions={0} | all-to-all | bytes 1179648 | tf_op jit(solution)/shard_map/all_to_all | solution.py:20
  29.9 0.9 all_to_all.31
  30.9 0.7 all-gather.7.cloned.1.call-update
  31.6 25.2 %all_to_all.37 = f32[16,32,768]{2,1,0:T(8,128)S(1)} all-to-all(f32[16,32,768]{2,1,0:T(8,128)S(1)} %copy-done.2), channel_id=1, replica_groups=mesh['layer'=2,'expert'=16,'matrix'=4] {'expert'}, dimensions={0} | all-to-all | bytes 3145728 | tf_op jit(solution)/shard_map/all_to_all | solution.py:19
  56.8 4.5 %all-to-all-start = ((f32[16,2048,32]{1,2,0:T(8,128)}), f32[16,2048,32]{1,2,0:T(8,128)}, u32[]{:S(2)}, u32[]{:S(2)}) async-start(f32[16,2048,32]{1,2,0:T(8,128)} %param.7), calls=%async_computation | async-start | bytes 8388608 | tf_op jit(solution)/shard_map/all_to_all | solution.py:17
  61.3 0.0 reduce-scatter.2.cloned.1.call-start
  61.4 1.3 broadcast_add_fusion
  62.7 2.4 reshape_squeeze.3
  65.1 2.0 copy.15
  67.2 2.6 reshape.43
  69.8 51.2 %all-to-all-done = f32[16,2048,32]{1,2,0:T(8,128)} async-done(((f32[16,2048,32]{1,2,0:T(8,128)}), f32[16,2048,32]{1,2,0:T(8,128)}, u32[]{:S(2)}, u32[]{:S(2)}) %all-to-all-start) | async-done | bytes 4194336 | tf_op jit(solution)/shard_map/all_to_all | solution.py:17
  121.0 9.2 %all-gather.7.cloned.1.call-done = f32[1,1,2048,768]{3,2,1,0:T(8,128)} async-done(((f32[1,1,512,768]{3,2,1,0:T(8,128)}), f32[1,1,2048,768]{3,2,1,0:T(8,128)}) %all-gather.7.cloned.1.call-update) | async-done | bytes 6291472 | tf_op jit(solution)/shard_map/all_gather | solution.py:34
  130.1 13.4 %fusion = f32[512,768]{1,0:T(8,128)S(1)} fusion(f32[2048,512]{0,1:T(8,128)} %bitcast.2, f32[1,1,2048,768]{3,2,1,0:T(8,128)} %all-gather.7.cloned.1.call-done), kind=kOutput, calls=%fused_computation | convolution fusion | flops 9663676416 | bytes 12058624 | tf_op jit(solution)/shard_map/ik,if->kf/dot_general | solution.py:31
  143.5 4.1 bitcast_divide_fusion
  147.6 4.0 fusion.4
  151.6 14.2 %convolution_bitcast_fusion = f32[2048,768]{0,1:T(8,128)} fusion(f32[512,768]{1,0:T(8,128)S(1)} %fusion.4, f32[2048,512]{0,1:T(8,128)} %bitcast.2), kind=kOutput, calls=%fused_computation.2 | convolution fusion | flops 9663676416 | bytes 12058624 | tf_op jit(solution)/shard_map/dot_general | solution.py:42
  165.8 1.4 copy-done
  167.2 0.5 copy.16
  168.9 61.7 %reduce-scatter.2.cloned.1.call-done = f32[512,768]{0,1:T(8,128)} async-done(((f32[2048,768]{0,1:T(8,128)}), f32[512,768]{0,1:T(8,128)}) %reduce-scatter.2.cloned.1.call-update) | async-done | bytes 1572880 | tf_op jit(solution)/shard_map/reduce_scatter | solution.py:44
  230.6 2.5 fusion.2
  233.1 1.6 copy.17
  235.5 174.4 %all-gather.1 = f32[64,1,32]{2,1,0:T(1,128)S(1)} all-gather(f32[1,1,32]{2,1,0:T(1,128)S(1)} %fusion.3), channel_id=1, replica_groups=mesh['layer'=2,'expert'=16,'matrix'=4] {'expert','matrix'}, dimensions={0}, use_global_device_ids=true | all-gather | bytes 8320 | tf_op jit(solution)/shard_map/all_gather | solution.py:56
  409.8 0.6 reduce_sum.20
  (11 shorter events, 0.1 us)
Async XLA Ops:
  7.2 55.5 %all-gather.5.cloned.1.call-start = ((), (), s32[]{:S(2)}) async-start(), calls=%async_computation.4 | async-start | bytes 2949120 | tf_op jit(solution)/shard_map/all_gather | solution.py:22
  29.9 1.7 copy-start.2
  30.9 99.2 %all-gather.7.cloned.1.call-start = ((), (), s32[]{:S(2)}) async-start(), calls=%async_computation.6 | async-start | bytes 7864320 | tf_op jit(solution)/shard_map/all_gather | solution.py:34
  56.8 64.2 %all-to-all-start = ((f32[16,2048,32]{1,2,0:T(8,128)}), f32[16,2048,32]{1,2,0:T(8,128)}, u32[]{:S(2)}, u32[]{:S(2)}) async-start(f32[16,2048,32]{1,2,0:T(8,128)} %param.7), calls=%async_computation | async-start | bytes 8388608 | tf_op jit(solution)/shard_map/all_to_all | solution.py:17
  61.3 169.3 %reduce-scatter.2.cloned.1.call-start = ((), (), s32[]{:S(2)}) async-start(), calls=%async_computation.5 | async-start | bytes 7864320 | tf_op jit(solution)/shard_map/reduce_scatter | solution.py:44
  130.1 13.4 %copy-start.1 = (f32[16,32,768]{2,1,0:T(8,128)S(1)}, f32[16,32,768]{2,1,0:T(8,128)}, u32[]{:S(2)}) copy-start(f32[16,32,768]{2,1,0:T(8,128)} %broadcast_add_fusion) | copy-start | bytes 4718596
  165.8 1.4 copy-start
Sparse Core Ops, SparseCore 0:
  31.0 31.6 all-gather.4
  64.3 65.7 all-gather.6
  165.9 64.6 reduce-scatter.1
